TPU v7x, 128 devices: a whole 4x4x4 slice. The times are simulated.
128 devices in a mesh: row: 8 (over z_lo, y), col: 16 (over z_hi, x, core).
Axes of the slice: x: 4, y: 4, z: 4 (z_hi: 2, z_lo: 2; z = z_hi * 2 + z_lo), core: 2. Of those that a mesh axis runs over, the one named last changes fastest.
Arguments:
- initial_field: float32 [256, 256, 256], P(('row', 'col')), may hold values from -5 to 5
Outputs:
- advanced_field: float32 [256, 256, 256], P(('row', 'col'))
All inputs are finite; a program needn't handle non-finite values.
Results may differ from a plain program's by a relative error of at most 0.0003.
Values sent between devices are 32-bit elements; how exact they have to be, the bound alone decides.
A program may use at most 64 MiB of HBM per device.

v0:
```python
import functools
import math

import jax
import jax.numpy as jnp
import numpy as np
from jax import lax
from jax.experimental import pallas as pl
from jax.experimental.pallas import tpu as pltpu
from jax.sharding import PartitionSpec as P

growth_rate = 0.3
quadratic = 1.0
time_step = 0.2
wave_scale = 4.0
MESH = pl.DeviceIdType.MESH
F32 = jnp.float32
BF16 = jnp.bfloat16


def basis(length):
    n = np.arange(length)
    half = length // 2
    mode = np.where(n <= half, n, n - half)
    angle = 2.0 * np.pi / length * ((mode[:, None] * n[None, :]) % length)
    table = np.where((n <= half)[:, None], np.cos(angle), np.sin(angle))
    scale = np.where((n == 0) | (n == half), 1.0 / length, 2.0 / length)
    return table * np.sqrt(scale)[:, None]


def split(value):
    high = value.astype(BF16)
    return high, (value - high.astype(F32)).astype(BF16)


def dot(left, right):
    return jnp.dot(left, right, preferred_element_type=F32)


def phi_values(argument):
    within = jnp.abs(argument) < 1.0
    inside = jnp.where(within, argument, 0.0)
    outside = jnp.where(within, 2.0, argument)
    series = []
    for degree in (1, 2, 3):
        running = jnp.zeros_like(argument) + 1.0 / math.factorial(11 + degree)
        for exponent in range(10, -1, -1):
            running = running * inside + 1.0 / math.factorial(exponent + degree)
        series.append(running)
    growth_term = jnp.exp(outside)
    closed_one = (growth_term - 1.0) / outside
    closed_two = (growth_term - 1.0 - outside) / (outside * outside)
    closed_three = (growth_term - 1.0 - outside - 0.5 * outside * outside) / (
        outside * outside * outside
    )
    return (
        jnp.where(within, series[0], closed_one),
        jnp.where(within, series[1], closed_two),
        jnp.where(within, series[2], closed_three),
    )


def step_factors(ksq):
    lin = growth_rate - (1.0 - ksq) * (1.0 - ksq)
    scaled = time_step * lin
    half_phi, _, _ = phi_values(0.5 * scaled)
    first_phi, second_phi, third_phi = phi_values(scaled)
    e_half = jnp.exp(0.5 * scaled)
    q_half = 0.5 * time_step * half_phi
    e_full = jnp.exp(scaled)
    f_one = time_step * (first_phi - 3.0 * second_phi + 4.0 * third_phi)
    f_two = time_step * (second_phi - 2.0 * third_phi)
    f_three = time_step * (4.0 * third_phi - second_phi)
    return (e_half, q_half, e_full, f_one, f_two, f_three)


def reaction(values):
    return quadratic * values * values - values * values * values


def wave(index, size):
    mode = jnp.where(index * 2 <= size, index, index - size // 2)
    return wave_scale * mode.astype(F32) / size


def kernel(
    sizes, offsets, field, qh_ref, ql_ref, th_ref, tl_ref, out_ref,
    send_f, recv_f, send_i, recv_i, held, factors,
    fsend, frecv, isend, irecv,
):
    rows, cols, size_x, size_y, size_z = sizes
    devices = rows * cols
    row = lax.axis_index("row")
    col = lax.axis_index("col")
    me = row * cols + col
    groups = size_y // 8
    count = devices - 1

    def peer(step):
        dr, dc = offsets(step, row, col)
        return dr, dc

    barrier = pltpu.get_barrier_semaphore()

    def greet(step, carry):
        pl.semaphore_signal(barrier, inc=1, device_id=peer(step), device_id_type=MESH)
        return carry

    lax.fori_loop(0, count, greet, 0)

    def tile(index):
        return pl.ds(pl.multiple_of(index * 8, 8), 8)

    def send(source, target, ssem, rsem):
        def one(step, carry):
            pr, pc = peer(step)
            pltpu.make_async_remote_copy(
                src_ref=source.at[tile(pr * cols + pc), :],
                dst_ref=target.at[tile(me), :],
                send_sem=ssem, recv_sem=rsem,
                device_id=(pr, pc), device_id_type=MESH,
            ).start()
            return carry

        lax.fori_loop(0, count, one, 0)
        target[tile(me), :] = source[tile(me), :]

    def drain(ref, sem):
        part = ref.at[pl.ds(0, count * 8), :]
        pltpu.make_async_copy(part, part, sem).wait()

    low = lax.broadcasted_iota(jnp.int32, (groups, 8, 128), 1) < 4

    def to_blocks(values, target):
        vh, vl = split(values)
        along_z = dot(vh, th_ref[...]) + dot(vl, th_ref[...]) + dot(vh, tl_ref[...])
        both = []
        for plane in range(2):
            wh, wl = split(along_z[plane * size_y : (plane + 1) * size_y])
            both.append(dot(qh_ref[...], wh) + dot(qh_ref[...], wl) + dot(ql_ref[...], wh))
        for part in range(2):
            a = both[0][:, part * 128 : part * 128 + 128].reshape(groups, 8, 128)
            b = both[1][:, part * 128 : part * 128 + 128].reshape(groups, 8, 128)
            first = jnp.where(low, a, pltpu.roll(b, 4, 1))
            second = jnp.where(low, pltpu.roll(a, 4, 1), b)
            base = part * 2 * size_y
            target[base : base + size_y, :] = first.reshape(size_y, 128)
            target[base + size_y : base + 2 * size_y, :] = second.reshape(size_y, 128)

    def from_blocks(source):
        planes = ([], [])
        for part in range(2):
            base = part * 2 * size_y
            first = source[base : base + size_y, :].reshape(groups, 8, 128)
            second = source[base + size_y : base + 2 * size_y, :].reshape(groups, 8, 128)
            a = jnp.where(low, first, pltpu.roll(second, 4, 1))
            b = jnp.where(low, pltpu.roll(first, 4, 1), second)
            planes[0].append(a.reshape(size_y, 128))
            planes[1].append(b.reshape(size_y, 128))
        done = []
        for plane in range(2):
            wh, wl = split(jnp.concatenate(planes[plane], axis=1))
            along_y = dot(th_ref[...], wh) + dot(th_ref[...], wl) + dot(tl_ref[...], wh)
            vh, vl = split(along_y)
            done.append(dot(vh, qh_ref[...]) + dot(vl, qh_ref[...]) + dot(vh, ql_ref[...]))
        return jnp.concatenate(done, axis=0)

    def gathered(source, pair):
        parts = [source[pl.ds(2 * pair + k, size_x, stride=4), :] for k in range(2)]
        gh, gl = split(jnp.concatenate(parts, axis=1))
        return dot(qh_ref[...], gh) + dot(qh_ref[...], gl) + dot(ql_ref[...], gh)

    def scattered(values, pair):
        vh, vl = split(values)
        along_x = dot(th_ref[...], vh) + dot(th_ref[...], vl) + dot(tl_ref[...], vh)
        for k in range(2):
            send_i[pl.ds(2 * pair + k, size_x, stride=4), :] = along_x[:, k * 128 : k * 128 + 128]

    values = field[...]
    to_blocks(values, send_f.at[0])
    pl.semaphore_wait(barrier, count)
    send(send_f.at[0], recv_f.at[0], fsend.at[0], frecv.at[0])
    to_blocks(reaction(values), send_f.at[1])
    send(send_f.at[1], recv_f.at[1], fsend.at[1], frecv.at[1])

    part = me // (devices // 2)
    half = (me // (devices // 4)) % 2
    group = me % (devices // 4)
    lane = lax.broadcasted_iota(jnp.int32, (8, 512), 1)
    ky = wave(group * 8 + half * 4 + lane // 128, size_y)
    kz = wave(part * 128 + lane % 128, size_z)
    kyz = ky * ky + kz * kz

    def factor_rows(block, carry):
        at = pl.ds(pl.multiple_of(block * 8, 8), 8)
        kx = wave(block * 8 + lax.broadcasted_iota(jnp.int32, (8, 512), 0), size_x)
        for index, value in enumerate(step_factors(kx * kx + kyz)):
            factors[index, at, :] = value
        return carry

    lax.fori_loop(0, size_x // 8, factor_rows, 0)

    E_HALF, Q_HALF, E_FULL, F_ONE, F_TWO, F_THREE = range(6)
    for pair in range(2):
        lanes = slice(pair * 256, pair * 256 + 256)
        if pair == 0:
            drain(recv_f.at[0], frecv.at[0])
            drain(recv_f.at[1], frecv.at[1])
        state = gathered(recv_f.at[0], pair)
        react_u = gathered(recv_f.at[1], pair)
        moved = factors[E_HALF, :, lanes] * state
        pushed = factors[Q_HALF, :, lanes] * react_u
        first = moved + pushed
        scattered(first, pair)
        held[0, :, lanes] = moved
        held[1, :, lanes] = factors[E_HALF, :, lanes] * first - pushed
        held[2, :, lanes] = factors[E_FULL, :, lanes] * state + factors[F_ONE, :, lanes] * react_u
    send(send_i, recv_i, isend, irecv)
    drain(send_f.at[0], fsend.at[0])
    drain(send_f.at[1], fsend.at[1])

    for stage in range(4):
        drain(recv_i, irecv)
        drain(send_i, isend)
        values = from_blocks(recv_i)
        if stage == 3:
            out_ref[...] = values
            break
        to_blocks(reaction(values), send_f.at[0])
        send(send_f.at[0], recv_f.at[0], fsend.at[0], frecv.at[0])
        drain(recv_f.at[0], frecv.at[0])
        drain(send_f.at[0], fsend.at[0])
        for pair in range(2):
            lanes = slice(pair * 256, pair * 256 + 256)
            react = gathered(recv_f.at[0], pair)
            if stage == 0:
                scattered(held[0, :, lanes] + factors[Q_HALF, :, lanes] * react, pair)
                held[2, :, lanes] += 2.0 * factors[F_TWO, :, lanes] * react
            if stage == 1:
                scattered(held[1, :, lanes] + 2.0 * (factors[Q_HALF, :, lanes] * react), pair)
                held[2, :, lanes] += 2.0 * factors[F_TWO, :, lanes] * react
            if stage == 2:
                scattered(held[2, :, lanes] + factors[F_THREE, :, lanes] * react, pair)
        send(send_i, recv_i, isend, irecv)


def schedule(step, row, col):
    def hop(code):
        return (2 + code + code // 2 + 2 * (code // 3)) % 4

    dz = hop(step // 32)
    dy = hop((step // 8) % 4)
    dx = hop((step // 2) % 4)
    dc = 1 - step % 2
    z = (col // 8) * 2 + row // 4
    y = row % 4
    x = (col // 2) % 4
    core = col % 2
    z = (z + dz) % 4
    y = (y + dy) % 4
    x = (x + dx) % 4
    core = (core + dc) % 2
    return (z % 2) * 4 + y, (z // 2) * 8 + x * 2 + core


def solution(mesh):
    rows, cols = mesh.shape["row"], mesh.shape["col"]
    table = basis(256).astype(np.float32)

    def halves(values):
        high = values.astype(BF16)
        return high, (values - high.astype(np.float32)).astype(BF16)

    qh, ql = halves(table)
    th, tl = halves(np.ascontiguousarray(table.T))

    def body(field):
        planes, size_y, size_z = field.shape
        size_x = planes * rows * cols
        sizes = (rows, cols, size_x, size_y, size_z)
        flat = field.reshape(planes * size_y, size_z)
        vmem = pl.BlockSpec(memory_space=pltpu.VMEM)
        out = pl.pallas_call(
            functools.partial(kernel, sizes, schedule),
            out_shape=jax.ShapeDtypeStruct(flat.shape, F32),
            in_specs=[vmem] * 5,
            out_specs=vmem,
            scratch_shapes=[
                pltpu.VMEM((2, size_x * 4, 128), F32),
                pltpu.VMEM((2, size_x * 4, 128), F32),
                pltpu.VMEM((size_x * 4, 128), F32),
                pltpu.VMEM((size_x * 4, 128), F32),
                pltpu.VMEM((3, size_x, 512), F32),
                pltpu.VMEM((6, size_x, 512), F32),
                pltpu.SemaphoreType.DMA((2,)),
                pltpu.SemaphoreType.DMA((2,)),
                pltpu.SemaphoreType.DMA,
                pltpu.SemaphoreType.DMA,
            ],
            compiler_params=pltpu.CompilerParams(
                collective_id=0, has_side_effects=True, vmem_limit_bytes=48 * 1024 * 1024
            ),
        )(flat, jnp.asarray(qh), jnp.asarray(ql), jnp.asarray(th), jnp.asarray(tl))
        return out.reshape(field.shape)

    placed = (P(("row", "col"), None, None),)
    return jax.shard_map(
        body, mesh=mesh, in_specs=placed, out_specs=P(("row", "col"), None, None), check_vma=False
    )
```

profile of v0, /device:TPU:1, one launch (start us, length us, event | category | flops | bytes accessed | tf_op | source)
XLA Modules:
  0.0 147.2 jit_solution(3073387405980972467)
XLA Ops:
  0.0 0.0 copy-start
  0.0 1.0 copy-done
  1.0 0.0 copy-start.1
  1.0 0.9 copy-done.1
  1.9 0.0 copy-start.2
  1.9 0.9 copy-done.2
  2.9 0.0 copy-start.3
  2.9 0.9 copy-done.3
  3.8 0.0 copy-start.4
  3.8 0.9 copy-done.4
  4.7 141.7 %shard_map.55 = f32[512,256]{1,0:T(8,128)S(1)} custom-call(f32[512,256]{1,0:T(8,128)S(1)} %bitcast.3, bf16[256,256]{1,0:T(8,128)(2,1)S(1)} %copy-done.4, bf16[256,256]{1,0:T(8,128)(2,1)S(1)} %copy-done.3, bf16[256,256]{1,0:T(8,128)(2,1)S(1)} %copy-done.2, bf16[256,256]{1,0:T(8,128)(2,1)S(1)} %copy-done.1), custom_call_target="tpu_custom_call" | custom-call | tf_op jit(solution)/shard_map/pallas_call | solution.py:283
  146.4 0.8 copy.7
Async XLA Ops:
  0.0 1.0 copy-start
  1.0 0.9 copy-start.1
  1.9 0.9 copy-start.2
  2.9 0.9 copy-start.3
  3.8 0.9 copy-start.4
where the time goes:
time: 147 us
  Pallas kernels  142 us (97%)
  local copies, waits for them, and re-layouts  5.45 us (4%)
    pallas_call x1, Pallas kernels, body(): pl.pallas_call(functools.partial(kernel, sizes, schedule), out_shape=jax....  142 us
    unnamed x11, local copies, waits for them, and re-layouts  5.45 us

commit v1 on v0

--- a/solution.py
+++ b/solution.py
@@ -13,7 +13,7 @@
 quadratic = 1.0
 time_step = 0.2
 wave_scale = 4.0
-MESH = pl.DeviceIdType.MESH
+LOGICAL = pl.DeviceIdType.LOGICAL
 F32 = jnp.float32
 BF16 = jnp.bfloat16
 
@@ -85,8 +85,8 @@
 
 def kernel(
     sizes, offsets, field, qh_ref, ql_ref, th_ref, tl_ref, out_ref,
-    send_f, recv_f, send_i, recv_i, held, factors,
-    fsend, frecv, isend, irecv,
+    send_p, recv_p, send_f, recv_f, send_i, recv_i, held, factors,
+    psend, precv, fsend, frecv, isend, irecv,
 ):
     rows, cols, size_x, size_y, size_z = sizes
     devices = rows * cols
@@ -96,37 +96,38 @@
     groups = size_y // 8
     count = devices - 1
 
-    def peer(step):
-        dr, dc = offsets(step, row, col)
-        return dr, dc
+    z, y = (col // 8) * 2 + row // 4, row % 4
+    x, core = (col // 2) % 4, col % 2
+    along_zy = {}
+    along_xc = {}
+    for far in range(4):
+        other = (z + far) % 4
+        base = (other % 2) * (4 * cols) + (other // 2) * 8
+        for near in range(4):
+            along_zy[far, near] = base + ((y + near) % 4) * cols
+        for near in range(2):
+            along_xc[far, near] = ((x + far) % 4) * 2 + (core + near) % 2
+    peers = [along_zy[o[0], o[1]] + along_xc[o[2], o[3]] for o in offsets]
 
     barrier = pltpu.get_barrier_semaphore()
-
-    def greet(step, carry):
-        pl.semaphore_signal(barrier, inc=1, device_id=peer(step), device_id_type=MESH)
-        return carry
-
-    lax.fori_loop(0, count, greet, 0)
+    for other in peers:
+        pl.semaphore_signal(barrier, inc=1, device_id=other, device_id_type=LOGICAL)
 
     def tile(index):
         return pl.ds(pl.multiple_of(index * 8, 8), 8)
 
     def send(source, target, ssem, rsem):
-        def one(step, carry):
-            pr, pc = peer(step)
+        for other in peers:
             pltpu.make_async_remote_copy(
-                src_ref=source.at[tile(pr * cols + pc), :],
-                dst_ref=target.at[tile(me), :],
+                src_ref=source.at[..., tile(other), :],
+                dst_ref=target.at[..., tile(me), :],
                 send_sem=ssem, recv_sem=rsem,
-                device_id=(pr, pc), device_id_type=MESH,
+                device_id=other, device_id_type=LOGICAL,
             ).start()
-            return carry
-
-        lax.fori_loop(0, count, one, 0)
-        target[tile(me), :] = source[tile(me), :]
+        target[..., tile(me), :] = source[..., tile(me), :]
 
     def drain(ref, sem):
-        part = ref.at[pl.ds(0, count * 8), :]
+        part = ref.at[..., pl.ds(0, count * 8), :]
         pltpu.make_async_copy(part, part, sem).wait()
 
     low = lax.broadcasted_iota(jnp.int32, (groups, 8, 128), 1) < 4
@@ -177,11 +178,10 @@
             send_i[pl.ds(2 * pair + k, size_x, stride=4), :] = along_x[:, k * 128 : k * 128 + 128]
 
     values = field[...]
-    to_blocks(values, send_f.at[0])
+    to_blocks(values, send_p.at[0])
+    to_blocks(reaction(values), send_p.at[1])
     pl.semaphore_wait(barrier, count)
-    send(send_f.at[0], recv_f.at[0], fsend.at[0], frecv.at[0])
-    to_blocks(reaction(values), send_f.at[1])
-    send(send_f.at[1], recv_f.at[1], fsend.at[1], frecv.at[1])
+    send(send_p, recv_p, psend, precv)
 
     part = me // (devices // 2)
     half = (me // (devices // 4)) % 2
@@ -204,10 +204,9 @@
     for pair in range(2):
         lanes = slice(pair * 256, pair * 256 + 256)
         if pair == 0:
-            drain(recv_f.at[0], frecv.at[0])
-            drain(recv_f.at[1], frecv.at[1])
-        state = gathered(recv_f.at[0], pair)
-        react_u = gathered(recv_f.at[1], pair)
+            drain(recv_p, precv)
+        state = gathered(recv_p.at[0], pair)
+        react_u = gathered(recv_p.at[1], pair)
         moved = factors[E_HALF, :, lanes] * state
         pushed = factors[Q_HALF, :, lanes] * react_u
         first = moved + pushed
@@ -216,8 +215,7 @@
         held[1, :, lanes] = factors[E_HALF, :, lanes] * first - pushed
         held[2, :, lanes] = factors[E_FULL, :, lanes] * state + factors[F_ONE, :, lanes] * react_u
     send(send_i, recv_i, isend, irecv)
-    drain(send_f.at[0], fsend.at[0])
-    drain(send_f.at[1], fsend.at[1])
+    drain(send_p, psend)
 
     for stage in range(4):
         drain(recv_i, irecv)
@@ -226,13 +224,13 @@
         if stage == 3:
             out_ref[...] = values
             break
-        to_blocks(reaction(values), send_f.at[0])
-        send(send_f.at[0], recv_f.at[0], fsend.at[0], frecv.at[0])
-        drain(recv_f.at[0], frecv.at[0])
-        drain(send_f.at[0], fsend.at[0])
+        to_blocks(reaction(values), send_f)
+        send(send_f, recv_f, fsend, frecv)
+        drain(recv_f, frecv)
+        drain(send_f, fsend)
         for pair in range(2):
             lanes = slice(pair * 256, pair * 256 + 256)
-            react = gathered(recv_f.at[0], pair)
+            react = gathered(recv_f, pair)
             if stage == 0:
                 scattered(held[0, :, lanes] + factors[Q_HALF, :, lanes] * react, pair)
                 held[2, :, lanes] += 2.0 * factors[F_TWO, :, lanes] * react
@@ -244,23 +242,13 @@
         send(send_i, recv_i, isend, irecv)
 
 
-def schedule(step, row, col):
-    def hop(code):
-        return (2 + code + code // 2 + 2 * (code // 3)) % 4
-
-    dz = hop(step // 32)
-    dy = hop((step // 8) % 4)
-    dx = hop((step // 2) % 4)
-    dc = 1 - step % 2
-    z = (col // 8) * 2 + row // 4
-    y = row % 4
-    x = (col // 2) % 4
-    core = col % 2
-    z = (z + dz) % 4
-    y = (y + dy) % 4
-    x = (x + dx) % 4
-    core = (core + dc) % 2
-    return (z % 2) * 4 + y, (z // 2) * 8 + x * 2 + core
+def hops(offset):
+    return sum(min(o, 4 - o) for o in offset[:3])
+
+
+def schedule():
+    every = [(a, b, c, d) for a in range(4) for b in range(4) for c in range(4) for d in range(2)]
+    return sorted(every[1:], key=lambda offset: -2 * hops(offset) - offset[3])
 
 
 def solution(mesh):
@@ -281,21 +269,17 @@
         flat = field.reshape(planes * size_y, size_z)
         vmem = pl.BlockSpec(memory_space=pltpu.VMEM)
         out = pl.pallas_call(
-            functools.partial(kernel, sizes, schedule),
+            functools.partial(kernel, sizes, schedule()),
             out_shape=jax.ShapeDtypeStruct(flat.shape, F32),
             in_specs=[vmem] * 5,
             out_specs=vmem,
             scratch_shapes=[
                 pltpu.VMEM((2, size_x * 4, 128), F32),
                 pltpu.VMEM((2, size_x * 4, 128), F32),
-                pltpu.VMEM((size_x * 4, 128), F32),
-                pltpu.VMEM((size_x * 4, 128), F32),
+                *[pltpu.VMEM((size_x * 4, 128), F32)] * 4,
                 pltpu.VMEM((3, size_x, 512), F32),
                 pltpu.VMEM((6, size_x, 512), F32),
-                pltpu.SemaphoreType.DMA((2,)),
-                pltpu.SemaphoreType.DMA((2,)),
-                pltpu.SemaphoreType.DMA,
-                pltpu.SemaphoreType.DMA,
+                *[pltpu.SemaphoreType.DMA] * 6,
             ],
             compiler_params=pltpu.CompilerParams(
                 collective_id=0, has_side_effects=True, vmem_limit_bytes=48 * 1024 * 1024

time: 147 us -> 102 us (0.69)
  Pallas kernels: 142 us -> 96.7 us
    pallas_call x1, Pallas kernels: 142 us -> 96.7 us  [body(): pl.pallas_call(functools.partial(kernel, sizes, schedule()), out_shape=ja...]
where the time goes in v1:
time: 102 us
  Pallas kernels  96.7 us (95%)
  local copies, waits for them, and re-layouts  5.45 us (5%)
    pallas_call x1, Pallas kernels, body(): pl.pallas_call(functools.partial(kernel, sizes, schedule()), out_shape=ja...  96.7 us
    unnamed x11, local copies, waits for them, and re-layouts  5.45 us

profile of v1, /device:TPU:1, one launch (start us, length us, event | category | flops | bytes accessed | tf_op | source)
XLA Modules:
  0.0 102.2 jit_solution(4086142390408155254)
XLA Ops:
  0.0 0.0 copy-start
  0.0 1.0 %copy-done = f32[2,256,256]{2,1,0:T(8,128)S(1)} copy-done((f32[2,256,256]{2,1,0:T(8,128)S(1)}, f32[2,256,256]{2,1,0:T(8,128)}, u32[]{:S(2)}) %copy-start) | copy-done | bytes 524312
  1.0 0.0 copy-start.1
  1.0 0.9 copy-done.1
  1.9 0.0 copy-start.2
  1.9 0.9 copy-done.2
  2.9 0.0 copy-start.3
  2.9 0.9 copy-done.3
  3.8 0.0 copy-start.4
  3.8 0.9 copy-done.4
  4.7 96.7 %shard_map.55 = f32[512,256]{1,0:T(8,128)S(1)} custom-call(f32[512,256]{1,0:T(8,128)S(1)} %bitcast.3, bf16[256,256]{1,0:T(8,128)(2,1)S(1)} %copy-done.4, bf16[256,256]{1,0:T(8,128)(2,1)S(1)} %copy-done.3, bf16[256,256]{1,0:T(8,128)(2,1)S(1)} %copy-done.2, bf16[256,256]{1,0:T(8,128)(2,1)S(1)} %copy-done.1), custom_call_target="tpu_custom_call" | custom-call | tf_op jit(solution)/shard_map/pallas_call | solution.py:271
  101.4 0.8 copy.7
Async XLA Ops:
  0.0 1.0 %copy-start = (f32[2,256,256]{2,1,0:T(8,128)S(1)}, f32[2,256,256]{2,1,0:T(8,128)}, u32[]{:S(2)}) copy-start(f32[2,256,256]{2,1,0:T(8,128)} %param.5) | copy-start | bytes 1572868
  1.0 0.9 copy-start.1
  1.9 0.9 copy-start.2
  2.9 0.9 copy-start.3
  3.8 0.9 copy-start.4

commit v2 on v1

v2 whole, which is shorter than its diff:
```python
import functools
import math

import jax
import jax.numpy as jnp
import numpy as np
from jax import lax
from jax.experimental import pallas as pl
from jax.experimental.pallas import tpu as pltpu
from jax.sharding import PartitionSpec as P

growth_rate = 0.3
quadratic = 1.0
time_step = 0.2
wave_scale = 4.0
LOGICAL = pl.DeviceIdType.LOGICAL
F32 = jnp.float32
BF16 = jnp.bfloat16


def basis(length):
    n = np.arange(length)
    half = length // 2
    mode = np.where(n <= half, n, n - half)
    angle = 2.0 * np.pi / length * ((mode[:, None] * n[None, :]) % length)
    table = np.where((n <= half)[:, None], np.cos(angle), np.sin(angle))
    scale = np.where((n == 0) | (n == half), 1.0 / length, 2.0 / length)
    return table * np.sqrt(scale)[:, None]


def split(value):
    high = value.astype(BF16)
    return high, (value - high.astype(F32)).astype(BF16)


def dot(left, right):
    return jnp.dot(left, right, preferred_element_type=F32)


def phi_values(argument):
    within = jnp.abs(argument) < 1.0
    inside = jnp.where(within, argument, 0.0)
    outside = jnp.where(within, 2.0, argument)
    series = []
    for degree in (1, 2, 3):
        running = jnp.zeros_like(argument) + 1.0 / math.factorial(11 + degree)
        for exponent in range(10, -1, -1):
            running = running * inside + 1.0 / math.factorial(exponent + degree)
        series.append(running)
    growth_term = jnp.exp(outside)
    closed_one = (growth_term - 1.0) / outside
    closed_two = (growth_term - 1.0 - outside) / (outside * outside)
    closed_three = (growth_term - 1.0 - outside - 0.5 * outside * outside) / (
        outside * outside * outside
    )
    return (
        jnp.where(within, series[0], closed_one),
        jnp.where(within, series[1], closed_two),
        jnp.where(within, series[2], closed_three),
    )


def step_factors(ksq):
    lin = growth_rate - (1.0 - ksq) * (1.0 - ksq)
    scaled = time_step * lin
    half_phi, _, _ = phi_values(0.5 * scaled)
    first_phi, second_phi, third_phi = phi_values(scaled)
    e_half = jnp.exp(0.5 * scaled)
    q_half = 0.5 * time_step * half_phi
    e_full = jnp.exp(scaled)
    f_one = time_step * (first_phi - 3.0 * second_phi + 4.0 * third_phi)
    f_two = time_step * (second_phi - 2.0 * third_phi)
    f_three = time_step * (4.0 * third_phi - second_phi)
    return (e_half, q_half, e_full, f_one, f_two, f_three)


def reaction(values):
    return quadratic * values * values - values * values * values


def wave(index, size):
    mode = jnp.where(index * 2 <= size, index, index - size // 2)
    return wave_scale * mode.astype(F32) / size


def kernel(
    sizes, offsets, field_hbm, qh_hbm, ql_hbm, th_hbm, tl_hbm, out_ref,
    field, qh_ref, ql_ref, th_ref, tl_ref,
    send_p, recv_p, send_f, recv_f, send_i, recv_i, held, factors,
    loaded, psend, precv, fsend, frecv, isend, irecv,
):
    rows, cols, size_x, size_y, size_z = sizes
    devices = rows * cols
    row = lax.axis_index("row")
    col = lax.axis_index("col")
    me = row * cols + col
    quarter = size_y // 4
    count = devices - 1

    z, y = (col // 8) * 2 + row // 4, row % 4
    x, core = (col // 2) % 4, col % 2
    along_zy = {}
    along_xc = {}
    for far in range(4):
        other = (z + far) % 4
        base = (other % 2) * (4 * cols) + (other // 2) * 8
        for near in range(4):
            along_zy[far, near] = base + ((y + near) % 4) * cols
        for near in range(2):
            along_xc[far, near] = ((x + far) % 4) * 2 + (core + near) % 2
    peers = [along_zy[o[0], o[1]] + along_xc[o[2], o[3]] for o in offsets]

    barrier = pltpu.get_barrier_semaphore()
    for other in peers:
        pl.semaphore_signal(barrier, inc=1, device_id=other, device_id_type=LOGICAL)

    loads = [
        pltpu.make_async_copy(source, target, loaded.at[index])
        for index, (source, target) in enumerate(
            ((field_hbm, field), (th_hbm, th_ref), (tl_hbm, tl_ref), (qh_hbm, qh_ref), (ql_hbm, ql_ref))
        )
    ]
    for load in loads:
        load.start()

    def tile(index):
        return pl.ds(pl.multiple_of(index * 4, 4), 4)

    def send(source, target, ssem, rsem):
        for other in peers:
            pltpu.make_async_remote_copy(
                src_ref=source.at[..., tile(other), :],
                dst_ref=target.at[..., tile(me), :],
                send_sem=ssem, recv_sem=rsem,
                device_id=other, device_id_type=LOGICAL,
            ).start()
        target[..., tile(me), :] = source[..., tile(me), :]

    def drain(ref, sem):
        part = ref.at[..., pl.ds(0, count * 4), :]
        pltpu.make_async_copy(part, part, sem).wait()

    def along_zf(values):
        vh, vl = split(values)
        moved = dot(vh, th_ref[...]) + dot(vl, th_ref[...]) + dot(vh, tl_ref[...])
        return split(jnp.concatenate([moved[:size_y], moved[size_y:]], axis=1))

    def along_yf(halves, chunk, target):
        wh, wl = halves
        at = slice(chunk * 2 * quarter, (chunk + 1) * 2 * quarter)
        moved = dot(qh_ref[at, :], wh) + dot(qh_ref[at, :], wl) + dot(ql_ref[at, :], wh)
        for plane in range(2):
            for part in range(2):
                lanes = slice(plane * size_z + part * 128, plane * size_z + part * 128 + 128)
                for k in range(2):
                    start = part * 4 * quarter + plane * 2 + k
                    target[pl.ds(start, quarter, stride=4), :] = moved[
                        k * quarter : (k + 1) * quarter, lanes
                    ]

    def along_yi(source, chunk):
        lines = []
        for k in range(2):
            across = []
            for plane in range(2):
                for part in range(2):
                    start = part * 4 * quarter + plane * 2 + k
                    across.append(source[pl.ds(start, quarter, stride=4), :])
            lines.append(jnp.concatenate(across, axis=1))
        wh, wl = split(jnp.concatenate(lines, axis=0))
        at = slice(chunk * 2 * quarter, (chunk + 1) * 2 * quarter)
        return dot(th_ref[:, at], wh) + dot(th_ref[:, at], wl) + dot(tl_ref[:, at], wh)

    def along_zi(moved):
        vh, vl = split(jnp.concatenate([moved[:, :size_z], moved[:, size_z:]], axis=0))
        return dot(vh, qh_ref[...]) + dot(vl, qh_ref[...]) + dot(vh, ql_ref[...])

    def gathered(source):
        parts = [source[pl.ds(k, size_x, stride=2), :] for k in range(2)]
        gh, gl = split(jnp.concatenate(parts, axis=1))
        return dot(qh_ref[...], gh) + dot(qh_ref[...], gl) + dot(ql_ref[...], gh)

    def scattered(values, target):
        vh, vl = split(values)
        moved = dot(th_ref[...], vh) + dot(th_ref[...], vl) + dot(tl_ref[...], vh)
        for k in range(2):
            target[pl.ds(k, size_x, stride=2), :] = moved[:, k * 128 : k * 128 + 128]

    for load in loads:
        load.wait()
    values = field[...]
    straight = along_zf(values)
    reacted = along_zf(reaction(values))
    for chunk in range(2):
        along_yf(straight, chunk, send_p.at[chunk, 0])
        along_yf(reacted, chunk, send_p.at[chunk, 1])
        if chunk == 0:
            pl.semaphore_wait(barrier, count)
        send(send_p.at[chunk], recv_p.at[chunk], psend.at[chunk], precv.at[chunk])

    part = me // (devices // 2)
    group = me % (devices // 2)
    lane = lax.broadcasted_iota(jnp.int32, (8, 512), 1)
    ky = wave((lane // 128) * quarter + group, size_y)
    kz = wave(part * 128 + lane % 128, size_z)
    kyz = ky * ky + kz * kz

    def factor_rows(block, carry):
        at = pl.ds(pl.multiple_of(block * 8, 8), 8)
        kx = wave(block * 8 + lax.broadcasted_iota(jnp.int32, (8, 512), 0), size_x)
        for index, value in enumerate(step_factors(kx * kx + kyz)):
            factors[index, at, :] = value
        return carry

    lax.fori_loop(0, size_x // 8, factor_rows, 0)

    E_HALF, Q_HALF, E_FULL, F_ONE, F_TWO, F_THREE = range(6)
    for chunk in range(2):
        lanes = slice(chunk * 256, chunk * 256 + 256)
        drain(recv_p.at[chunk], precv.at[chunk])
        state = gathered(recv_p.at[chunk, 0])
        react_u = gathered(recv_p.at[chunk, 1])
        moved = factors[E_HALF, :, lanes] * state
        pushed = factors[Q_HALF, :, lanes] * react_u
        first = moved + pushed
        scattered(first, send_i.at[chunk])
        send(send_i.at[chunk], recv_i.at[chunk], isend.at[chunk], irecv.at[chunk])
        held[0, :, lanes] = moved
        held[1, :, lanes] = factors[E_HALF, :, lanes] * first - pushed
        held[2, :, lanes] = factors[E_FULL, :, lanes] * state + factors[F_ONE, :, lanes] * react_u
    for chunk in range(2):
        drain(send_p.at[chunk], psend.at[chunk])

    for stage in range(4):
        drain(recv_i.at[0], irecv.at[0])
        moved = along_yi(recv_i.at[0], 0)
        drain(recv_i.at[1], irecv.at[1])
        values = along_zi(moved + along_yi(recv_i.at[1], 1))
        for chunk in range(2):
            drain(send_i.at[chunk], isend.at[chunk])
        if stage == 3:
            out_ref[...] = values
            break
        halves = along_zf(reaction(values))
        for chunk in range(2):
            along_yf(halves, chunk, send_f.at[chunk])
            send(send_f.at[chunk], recv_f.at[chunk], fsend.at[chunk], frecv.at[chunk])
        for chunk in range(2):
            lanes = slice(chunk * 256, chunk * 256 + 256)
            drain(recv_f.at[chunk], frecv.at[chunk])
            react = gathered(recv_f.at[chunk])
            if stage == 0:
                spectrum = held[0, :, lanes] + factors[Q_HALF, :, lanes] * react
            if stage == 1:
                spectrum = held[1, :, lanes] + 2.0 * (factors[Q_HALF, :, lanes] * react)
            if stage == 2:
                spectrum = held[2, :, lanes] + factors[F_THREE, :, lanes] * react
            scattered(spectrum, send_i.at[chunk])
            send(send_i.at[chunk], recv_i.at[chunk], isend.at[chunk], irecv.at[chunk])
            if stage < 2:
                held[2, :, lanes] += 2.0 * factors[F_TWO, :, lanes] * react
        for chunk in range(2):
            drain(send_f.at[chunk], fsend.at[chunk])


def hops(offset):
    return sum(min(o, 4 - o) for o in offset[:3])


def schedule():
    every = [(a, b, c, d) for a in range(4) for b in range(4) for c in range(4) for d in range(2)]
    return sorted(every[1:], key=lambda offset: -2 * hops(offset) - offset[3])


def solution(mesh):
    rows, cols = mesh.shape["row"], mesh.shape["col"]
    table = basis(256).astype(np.float32)

    def halves(values):
        high = values.astype(BF16)
        return high, (values - high.astype(np.float32)).astype(BF16)

    qh, ql = halves(table)
    th, tl = halves(np.ascontiguousarray(table.T))

    def body(field):
        planes, size_y, size_z = field.shape
        size_x = planes * rows * cols
        sizes = (rows, cols, size_x, size_y, size_z)
        flat = field.reshape(planes * size_y, size_z)
        hbm = pl.BlockSpec(memory_space=pltpu.HBM)
        tables = [pltpu.VMEM(table.shape, BF16)] * 4
        out = pl.pallas_call(
            functools.partial(kernel, sizes, schedule()),
            out_shape=jax.ShapeDtypeStruct(flat.shape, F32),
            in_specs=[hbm] * 5,
            out_specs=pl.BlockSpec(memory_space=pltpu.VMEM),
            scratch_shapes=[
                pltpu.VMEM(flat.shape, F32),
                *tables,
                *[pltpu.VMEM((2, 2, size_x * 2, 128), F32)] * 2,
                *[pltpu.VMEM((2, size_x * 2, 128), F32)] * 4,
                pltpu.VMEM((3, size_x, 512), F32),
                pltpu.VMEM((6, size_x, 512), F32),
                pltpu.SemaphoreType.DMA((5,)),
                *[pltpu.SemaphoreType.DMA((2,))] * 6,
            ],
            compiler_params=pltpu.CompilerParams(
                collective_id=0, has_side_effects=True, vmem_limit_bytes=67043328
            ),
        )(flat, jnp.asarray(qh), jnp.asarray(ql), jnp.asarray(th), jnp.asarray(tl))
        return out.reshape(field.shape)

    placed = (P(("row", "col"), None, None),)
    return jax.shard_map(
        body, mesh=mesh, in_specs=placed, out_specs=P(("row", "col"), None, None), check_vma=False
    )
```

time: 102 us -> 94.8 us (0.929)
  Pallas kernels: 96.7 us -> 92.8 us
  local copies, waits for them, and re-layouts: 5.45 us -> 1.87 us
    pallas_call x1, Pallas kernels: 96.7 us -> 92.8 us  [body(): pl.pallas_call(functools.partial(kernel, sizes, schedule()), out_shape=ja...]
    unnamed x11 -> x1, local copies, waits for them, and re-layouts: 5.45 us -> 1.87 us
where the time goes in v2:
time: 94.8 us; the launch traced here: 94.6 us
  Pallas kernels  92.8 us (98%)
  local copies, waits for them, and re-layouts  1.87 us (2%)
    pallas_call x1, Pallas kernels, body(): pl.pallas_call(functools.partial(kernel, sizes, schedule()), out_shape=ja...  92.8 us

profile of v2, /device:TPU:1, one launch (start us, length us, event | category | flops | bytes accessed | tf_op | source)
XLA Modules:
  0.0 94.6 jit_solution(18121468232925789492)
XLA Ops:
  0.0 92.8 %shard_map.55 = f32[512,256]{1,0:T(8,128)} custom-call(f32[512,256]{1,0:T(8,128)} %bitcast.3, bf16[256,256]{1,0:T(8,128)(2,1)} %constant.8.clone.qh_hbm, bf16[256,256]{1,0:T(8,128)(2,1)} %constant.9.clone.ql_hbm, bf16[256,256]{1,0:T(8,128)(2,1)} %constant.10.clone.th_hbm, bf16[256,256]{1,0:T(8,128)(2,1)} %constant.11.clone.tl_hbm), custom_call_target="tpu_custom_call" | custom-call | tf_op jit(solution)/shard_map/pallas_call | solution.py:293
  92.8 1.9 %copy.7 = f32[2,256,256]{2,1,0:T(8,128)} copy(f32[2,256,256]{2,1,0:T(8,128)} %bitcast.2) | data formatting | bytes 1048576

commit v3 on v2

--- a/solution.py
+++ b/solution.py
@@ -292,7 +292,7 @@
         tables = [pltpu.VMEM(table.shape, BF16)] * 4
         out = pl.pallas_call(
             functools.partial(kernel, sizes, schedule()),
-            out_shape=jax.ShapeDtypeStruct(flat.shape, F32),
+            out_shape=pltpu.VMEM(flat.shape, F32),
             in_specs=[hbm] * 5,
             out_specs=pl.BlockSpec(memory_space=pltpu.VMEM),
             scratch_shapes=[
@@ -306,7 +306,7 @@
                 *[pltpu.SemaphoreType.DMA((2,))] * 6,
             ],
             compiler_params=pltpu.CompilerParams(
-                collective_id=0, has_side_effects=True, vmem_limit_bytes=67043328
+                collective_id=0, has_side_effects=True, vmem_limit_bytes=66000000
             ),
         )(flat, jnp.asarray(qh), jnp.asarray(ql), jnp.asarray(th), jnp.asarray(tl))
         return out.reshape(field.shape)

time: 94.8 us -> 92.9 us (0.980)
  local copies, waits for them, and re-layouts: 1.87 us -> 0.8 us
    unnamed x1, local copies, waits for them, and re-layouts: 1.87 us -> 0.8 us
where the time goes in v3:
time: 92.9 us; the launch traced here: 92.8 us
  Pallas kernels  91.9 us (99%)
    pallas_call x1, Pallas kernels, body(): pl.pallas_call(functools.partial(kernel, sizes, schedule()), out_shape=pl...  91.9 us

profile of v3, /device:TPU:1, one launch (start us, length us, event | category | flops | bytes accessed | tf_op | source)
XLA Modules:
  0.0 92.8 jit_solution(9398301670100678218)
XLA Ops:
  0.0 91.9 %shard_map.55 = f32[512,256]{1,0:T(8,128)S(1)} custom-call(f32[512,256]{1,0:T(8,128)} %bitcast.3, bf16[256,256]{1,0:T(8,128)(2,1)} %constant.8.clone.qh_hbm, bf16[256,256]{1,0:T(8,128)(2,1)} %constant.9.clone.ql_hbm, bf16[256,256]{1,0:T(8,128)(2,1)} %constant.10.clone.th_hbm, bf16[256,256]{1,0:T(8,128)(2,1)} %constant.11.clone.tl_hbm), custom_call_target="tpu_custom_call" | custom-call | tf_op jit(solution)/shard_map/pallas_call | solution.py:293
  92.0 0.8 copy.7

commit v4 on v3

--- a/solution.py
+++ b/solution.py
@@ -298,8 +298,8 @@
             scratch_shapes=[
                 pltpu.VMEM(flat.shape, F32),
                 *tables,
-                *[pltpu.VMEM((2, 2, size_x * 2, 128), F32)] * 2,
-                *[pltpu.VMEM((2, size_x * 2, 128), F32)] * 4,
+                *[pltpu.VMEM((2, 2, size_x * 2 + 8, 128), F32)] * 2,
+                *[pltpu.VMEM((2, size_x * 2 + 8, 128), F32)] * 4,
                 pltpu.VMEM((3, size_x, 512), F32),
                 pltpu.VMEM((6, size_x, 512), F32),
                 pltpu.SemaphoreType.DMA((5,)),

time: 92.9 us -> 92.6 us (level)
  no operation moved by 1% of the time
where the time goes in v4:
time: 92.6 us; the launch traced here: 92.4 us
  Pallas kernels  91.6 us (99%)
    pallas_call x1, Pallas kernels, body(): pl.pallas_call(functools.partial(kernel, sizes, schedule()), out_shape=pl...  91.6 us

profile of v4, /device:TPU:1, one launch (start us, length us, event | category | flops | bytes accessed | tf_op | source)
XLA Modules:
  0.0 92.4 jit_solution(8420645439820936935)
XLA Ops:
  0.0 91.6 %shard_map.55 = f32[512,256]{1,0:T(8,128)S(1)} custom-call(f32[512,256]{1,0:T(8,128)} %bitcast.3, bf16[256,256]{1,0:T(8,128)(2,1)} %constant.8.clone.qh_hbm, bf16[256,256]{1,0:T(8,128)(2,1)} %constant.9.clone.ql_hbm, bf16[256,256]{1,0:T(8,128)(2,1)} %constant.10.clone.th_hbm, bf16[256,256]{1,0:T(8,128)(2,1)} %constant.11.clone.tl_hbm), custom_call_target="tpu_custom_call" | custom-call | tf_op jit(solution)/shard_map/pallas_call | solution.py:293
  91.6 0.8 copy.7

commit v5 on v4

v5 whole, which is shorter than its diff:
```python
import functools
import math

import jax
import jax.numpy as jnp
import numpy as np
from jax import lax
from jax.experimental import pallas as pl
from jax.experimental.pallas import tpu as pltpu
from jax.sharding import PartitionSpec as P

growth_rate = 0.3
quadratic = 1.0
time_step = 0.2
wave_scale = 4.0
LOGICAL = pl.DeviceIdType.LOGICAL
F32 = jnp.float32
BF16 = jnp.bfloat16


def basis(length):
    n = np.arange(length)
    half = length // 2
    mode = np.where(n <= half, n, n - half)
    angle = 2.0 * np.pi / length * ((mode[:, None] * n[None, :]) % length)
    table = np.where((n <= half)[:, None], np.cos(angle), np.sin(angle))
    scale = np.where((n == 0) | (n == half), 1.0 / length, 2.0 / length)
    return table * np.sqrt(scale)[:, None]


def split(value):
    high = value.astype(BF16)
    return high, (value - high.astype(F32)).astype(BF16)


def dot(left, right):
    return jnp.dot(left, right, preferred_element_type=F32)


def phi_values(argument):
    within = jnp.abs(argument) < 1.0
    inside = jnp.where(within, argument, 0.0)
    outside = jnp.where(within, 2.0, argument)
    series = []
    for degree in (1, 2, 3):
        running = jnp.zeros_like(argument) + 1.0 / math.factorial(11 + degree)
        for exponent in range(10, -1, -1):
            running = running * inside + 1.0 / math.factorial(exponent + degree)
        series.append(running)
    growth_term = jnp.exp(outside)
    closed_one = (growth_term - 1.0) / outside
    closed_two = (growth_term - 1.0 - outside) / (outside * outside)
    closed_three = (growth_term - 1.0 - outside - 0.5 * outside * outside) / (
        outside * outside * outside
    )
    return (
        jnp.where(within, series[0], closed_one),
        jnp.where(within, series[1], closed_two),
        jnp.where(within, series[2], closed_three),
    )


def step_factors(ksq):
    lin = growth_rate - (1.0 - ksq) * (1.0 - ksq)
    scaled = time_step * lin
    half_phi, _, _ = phi_values(0.5 * scaled)
    first_phi, second_phi, third_phi = phi_values(scaled)
    e_half = jnp.exp(0.5 * scaled)
    q_half = 0.5 * time_step * half_phi
    e_full = jnp.exp(scaled)
    f_one = time_step * (first_phi - 3.0 * second_phi + 4.0 * third_phi)
    f_two = time_step * (second_phi - 2.0 * third_phi)
    f_three = time_step * (4.0 * third_phi - second_phi)
    return (e_half, q_half, e_full, f_one, f_two, f_three)


def reaction(values):
    return quadratic * values * values - values * values * values


def wave(index, size):
    mode = jnp.where(index * 2 <= size, index, index - size // 2)
    return wave_scale * mode.astype(F32) / size


def kernel(
    sizes, offsets, field_hbm, tables_hbm, out_ref, field, tables,
    send_p0, recv_p0, send_p1, recv_p1, send_f0, recv_f0, send_f1, recv_f1,
    send_i0, recv_i0, send_i1, recv_i1, held, gains,
    loaded, psend, precv, fsend, frecv, isend, irecv,
):
    rows, cols, size_x, size_y, size_z = sizes
    devices = rows * cols
    row = lax.axis_index("row")
    col = lax.axis_index("col")
    me = row * cols + col
    quarter = size_y // 4
    count = devices - 1

    z, y = (col // 8) * 2 + row // 4, row % 4
    x, core = (col // 2) % 4, col % 2
    along_zy = {}
    along_xc = {}
    for far in range(4):
        other = (z + far) % 4
        base = (other % 2) * (4 * cols) + (other // 2) * 8
        for near in range(4):
            along_zy[far, near] = base + ((y + near) % 4) * cols
        for near in range(2):
            along_xc[far, near] = ((x + far) % 4) * 2 + (core + near) % 2
    peers = [along_zy[o[0], o[1]] + along_xc[o[2], o[3]] for o in offsets]

    barrier = pltpu.get_barrier_semaphore()
    for other in peers:
        pl.semaphore_signal(barrier, inc=1, device_id=other, device_id_type=LOGICAL)

    loads = [
        pltpu.make_async_copy(field_hbm, field, loaded.at[0]),
        pltpu.make_async_copy(tables_hbm, tables, loaded.at[1]),
    ]
    qh_ref, ql_ref, th_ref, tl_ref, xqh_ref, xql_ref, xth_ref, xtl_ref = (
        tables.at[index] for index in range(8)
    )
    for load in loads:
        load.start()

    def send(source, target, ssem, rsem):
        depth = source.shape[0] // devices

        def tile(index):
            return pl.ds(pl.multiple_of(index * depth, depth), depth)

        for other in peers:
            pltpu.make_async_remote_copy(
                src_ref=source.at[tile(other), :],
                dst_ref=target.at[tile(me), :],
                send_sem=ssem, recv_sem=rsem,
                device_id=other, device_id_type=LOGICAL,
            ).start()
        target[tile(me), :] = source[tile(me), :]

    def drain(ref, sem):
        part = ref.at[pl.ds(0, count * (ref.shape[0] // devices)), :]
        pltpu.make_async_copy(part, part, sem).wait()

    def first_rows(whole, cut, entry):
        def at(plane, chunk, k):
            if plane == 0:
                return whole, 8, entry * 4 + chunk * 2 + k
            return cut.at[chunk], 4, entry * 2 + k

        return at

    def forward_rows(whole, cut):
        def at(plane, chunk, k):
            return (cut.at[chunk], 2, k) if plane else (whole, 4, chunk * 2 + k)

        return at

    def inverse_rows(whole, cut):
        def at(plane, chunk, k):
            return (whole, 4, chunk * 2 + k) if plane else (cut.at[chunk], 2, k)

        return at

    def lines_of(place, start, length):
        ref, depth, row_in = place
        return ref, pl.ds(start * depth + row_in, length, stride=depth)

    def read(place, start, length):
        ref, at = lines_of(place, start, length)
        return ref[at, :]

    def write(place, start, length, values):
        ref, at = lines_of(place, start, length)
        ref[at, :] = values

    def send_first(index):
        if index == 0:
            send(send_p0, recv_p0, psend.at[0], precv.at[0])
        else:
            send(send_p1.at[index - 1], recv_p1.at[index - 1], psend.at[index], precv.at[index])

    def send_forward(index):
        if index == 0:
            send(send_f0, recv_f0, fsend.at[0], frecv.at[0])
        else:
            send(send_f1.at[index - 1], recv_f1.at[index - 1], fsend.at[index], frecv.at[index])

    def send_inverse(index):
        if index == 2:
            send(send_i0, recv_i0, isend.at[2], irecv.at[2])
        else:
            send(send_i1.at[index], recv_i1.at[index], isend.at[index], irecv.at[index])

    def finish_first(index, whole, cut, sem):
        drain(whole if index == 0 else cut.at[index - 1], sem.at[index])

    def finish_inverse(index, whole, cut, sem):
        drain(whole if index == 2 else cut.at[index], sem.at[index])

    def along_zf(values):
        vh, vl = split(values)
        return split(dot(vh, th_ref[...]) + dot(vl, th_ref[...]) + dot(vh, tl_ref[...]))

    def along_yf(halves, plane, chunk, place):
        wh, wl = halves
        at = slice(chunk * 2 * quarter, (chunk + 1) * 2 * quarter)
        moved = dot(qh_ref[at, :], wh) + dot(qh_ref[at, :], wl) + dot(ql_ref[at, :], wh)
        for part in range(2):
            for k in range(2):
                lanes = slice(part * 128, part * 128 + 128)
                values = moved[k * quarter : (k + 1) * quarter, lanes]
                write(place(plane, chunk, k), part * quarter, quarter, values)

    def physical(plane):
        lines = []
        place = inverse_rows(recv_i0, recv_i1)
        for chunk in range(2):
            for k in range(2):
                across = [read(place(plane, chunk, k), part * quarter, quarter) for part in range(2)]
                lines.append(jnp.concatenate(across, axis=1))
        wh, wl = split(jnp.concatenate(lines, axis=0))
        moved = dot(th_ref[...], wh) + dot(th_ref[...], wl) + dot(tl_ref[...], wh)
        vh, vl = split(moved)
        return dot(vh, qh_ref[...]) + dot(vl, qh_ref[...]) + dot(vh, ql_ref[...])

    def gathered(place, chunk):
        lines = []
        for plane in range(2):
            across = [read(place(plane, chunk, k), 0, size_x // 2) for k in range(2)]
            lines.append(jnp.concatenate(across, axis=1))
        gh, gl = split(jnp.concatenate(lines, axis=0))
        return dot(xqh_ref[...], gh) + dot(xqh_ref[...], gl) + dot(xql_ref[...], gh)

    def scattered(values, chunk):
        vh, vl = split(values)
        moved = dot(xth_ref[...], vh) + dot(xth_ref[...], vl) + dot(xtl_ref[...], vh)
        for plane in range(2):
            rows_x = slice(plane * (size_x // 2), (plane + 1) * (size_x // 2))
            for k in range(2):
                place = inverse_rows(send_i0, send_i1)(plane, chunk, k)
                write(place, 0, size_x // 2, moved[rows_x, k * 128 : k * 128 + 128])

    for load in loads:
        load.wait()
    for plane in range(2):
        values = field[plane * size_y : (plane + 1) * size_y, :]
        straight = along_zf(values)
        reacted = along_zf(reaction(values))
        for chunk in range(2):
            at = plane * 2 + chunk
            along_yf(straight, plane, chunk, first_rows(send_p0, send_p1, 0))
            along_yf(reacted, plane, chunk, first_rows(send_p0, send_p1, 1))
            if at == 1:
                pl.semaphore_wait(barrier, count)
            if at > 0:
                send_first(at - 1)

    part = me // (devices // 2)
    group = me % (devices // 2)
    lane = lax.broadcasted_iota(jnp.int32, (8, 512), 1)
    ky = wave((lane // 128) * quarter + group, size_y)
    kz = wave(part * 128 + lane % 128, size_z)
    kyz = ky * ky + kz * kz

    def factor_rows(block, carry):
        at = pl.ds(pl.multiple_of(block * 8, 8), 8)
        kx = wave(block * 8 + lax.broadcasted_iota(jnp.int32, (8, 512), 0), size_x)
        e_half, q_half, e_full, f_one, f_two, f_three = step_factors(kx * kx + kyz)
        gains[0, at, :] = q_half
        gains[1, at, :] = 2.0 * q_half
        gains[2, at, :] = f_three
        gains[3, at, :] = 2.0 * f_two
        gains[4, at, :] = e_half
        gains[5, at, :] = e_full
        gains[6, at, :] = f_one
        return carry

    lax.fori_loop(0, size_x // 8, factor_rows, 0)

    finish_first(0, recv_p0, recv_p1, precv)
    known = []
    for chunk in range(2):
        lanes = slice(chunk * 256, chunk * 256 + 256)
        finish_first(1 + chunk, recv_p0, recv_p1, precv)
        state = gathered(first_rows(recv_p0, recv_p1, 0), chunk)
        react_u = gathered(first_rows(recv_p0, recv_p1, 1), chunk)
        moved = gains[4, :, lanes] * state
        pushed = gains[0, :, lanes] * react_u
        scattered(moved + pushed, chunk)
        send_inverse(chunk)
        known.append((lanes, state, react_u, moved, pushed))
    send_inverse(2)
    for lanes, state, react_u, moved, pushed in known:
        held[0, :, lanes] = moved
        held[1, :, lanes] = gains[4, :, lanes] * (moved + pushed) - pushed
        held[2, :, lanes] = gains[5, :, lanes] * state + gains[6, :, lanes] * react_u
    for index in range(3):
        finish_first(index, send_p0, send_p1, psend)

    def arrived(plane):
        for index in (0, 1) if plane == 0 else (2,):
            finish_inverse(index, recv_i0, recv_i1, irecv)

    def stage(index, carry):
        for plane in range(2):
            arrived(plane)
            halves = along_zf(reaction(physical(plane)))
            for chunk in range(2):
                at = plane * 2 + chunk
                along_yf(halves, plane, chunk, forward_rows(send_f0, send_f1))
                if at > 0:
                    send_forward(at - 1)
        for part in range(3):
            finish_inverse(part, send_i0, send_i1, isend)
        finish_first(0, recv_f0, recv_f1, frecv)
        known = []
        for chunk in range(2):
            lanes = slice(chunk * 256, chunk * 256 + 256)
            finish_first(1 + chunk, recv_f0, recv_f1, frecv)
            react = gathered(forward_rows(recv_f0, recv_f1), chunk)
            scattered(held[index, :, lanes] + gains[index, :, lanes] * react, chunk)
            send_inverse(chunk)
            known.append((lanes, react))
        send_inverse(2)
        for lanes, react in known:
            held[2, :, lanes] += gains[3, :, lanes] * react
        for part in range(3):
            finish_first(part, send_f0, send_f1, fsend)
        return carry

    lax.fori_loop(0, 3, stage, 0)
    for plane in range(2):
        arrived(plane)
        out_ref[plane * size_y : (plane + 1) * size_y, :] = physical(plane)
    for part in range(3):
        finish_inverse(part, send_i0, send_i1, isend)


def hops(offset):
    return sum(min(o, 4 - o) for o in offset[:3])


def schedule():
    every = [(a, b, c, d) for a in range(4) for b in range(4) for c in range(4) for d in range(2)]
    return sorted(every[1:], key=lambda offset: -2 * hops(offset) - offset[3])


def solution(mesh):
    rows, cols = mesh.shape["row"], mesh.shape["col"]
    table = basis(256).astype(np.float32)

    def halves(values):
        high = values.astype(BF16)
        return high, (values - high.astype(np.float32)).astype(BF16)

    along_x = np.concatenate([table[:, 0::2], table[:, 1::2]], axis=1)
    tables = np.stack([h for t in (table, table.T, along_x, along_x.T) for h in halves(t)])

    def body(field):
        planes, size_y, size_z = field.shape
        size_x = planes * rows * cols
        sizes = (rows, cols, size_x, size_y, size_z)
        flat = field.reshape(planes * size_y, size_z)
        hbm = pl.BlockSpec(memory_space=pltpu.HBM)
        out = pl.pallas_call(
            functools.partial(kernel, sizes, schedule()),
            out_shape=pltpu.VMEM(flat.shape, F32),
            in_specs=[hbm] * 2,
            out_specs=pl.BlockSpec(memory_space=pltpu.VMEM),
            scratch_shapes=[
                pltpu.VMEM(flat.shape, F32),
                pltpu.VMEM(tables.shape, BF16),
                *[pltpu.VMEM((size_x * 4 + 8, 128), F32)] * 2,
                *[pltpu.VMEM((2, size_x * 2 + 8, 128), F32)] * 2,
                *[pltpu.VMEM((size_x * 2 + 8, 128), F32)] * 2,
                *[pltpu.VMEM((2, size_x + 8, 128), F32)] * 2,
                *[pltpu.VMEM((size_x * 2 + 8, 128), F32)] * 2,
                *[pltpu.VMEM((2, size_x + 8, 128), F32)] * 2,
                pltpu.VMEM((3, size_x, 512), F32),
                pltpu.VMEM((7, size_x, 512), F32),
                pltpu.SemaphoreType.DMA((2,)),
                *[pltpu.SemaphoreType.DMA((3,))] * 6,
            ],
            compiler_params=pltpu.CompilerParams(
                collective_id=0, has_side_effects=True, vmem_limit_bytes=66000000
            ),
        )(flat, jnp.asarray(tables))
        return out.reshape(field.shape)

    placed = (P(("row", "col"), None, None),)
    return jax.shard_map(
        body, mesh=mesh, in_specs=placed, out_specs=P(("row", "col"), None, None), check_vma=False
    )
```

time: 92.6 us -> 92.7 us (level)
  no operation moved by 1% of the time
where the time goes in v5:
time: 92.7 us; the launch traced here: 92.5 us
  Pallas kernels  91.7 us (99%)
    pallas_call x1, Pallas kernels, body(): pl.pallas_call(functools.partial(kernel, sizes, schedule()), out_shape=pl...  91.7 us

profile of v5, /device:TPU:1, one launch (start us, length us, event | category | flops | bytes accessed | tf_op | source)
XLA Modules:
  0.0 92.5 jit_solution(1305259987847301819)
XLA Ops:
  0.0 91.7 %shard_map.28 = f32[512,256]{1,0:T(8,128)S(1)} custom-call(f32[512,256]{1,0:T(8,128)} %bitcast.3, bf16[8,256,256]{2,1,0:T(8,128)(2,1)} %constant.2.clone.tables_hbm), custom_call_target="tpu_custom_call" | custom-call | tf_op jit(solution)/shard_map/pallas_call | solution.py:367
  91.7 0.8 copy.4
